TPU v7x, 32 devices: a whole 2x2x4 slice. The times are simulated.
32 devices in a mesh: dp: 8 (over y, x, core), vocab: 4 (over z).
Axes of the slice: x: 2, y: 2, z: 4, core: 2. Of those that a mesh axis runs over, the one named last changes fastest.
Arguments:
- resid: bfloat16 [2, 1024, 4096], P(None, 'dp'), may hold values from -6 to 6
- norm_gain: float32 [4096], replicated, may hold values from 0.5 to 1.5
- in_x: bfloat16 [4096, 4096], P('dp', 'vocab'), may hold values from -0.09375 to 0.09375
- in_z: bfloat16 [4096, 4096], P('dp', 'vocab'), may hold values from -0.09375 to 0.09375
- conv_w: float32 [4, 4096], P(None, 'vocab'), may hold values from -3 to 3
- conv_b: float32 [4096], P('vocab'), may hold values from -3 to 3
- xdt_w: bfloat16 [4096, 256], P('vocab'), may hold values from -0.09375 to 0.09375
- xbc_w: bfloat16 [4096, 32], P('vocab'), may hold values from -0.09375 to 0.09375
- dt_gain: float32 [256], replicated, may hold values from 0.5 to 1.5
- dt_proj: bfloat16 [256, 4096], P(None, 'vocab'), may hold values from -0.375 to 0.375
- dt_bias: float32 [4096], P('vocab'), may hold values from -4 to 1
- a_rate: float32 [4096, 16], P('vocab'), may hold values from 0.0001 to 1
- out_w: bfloat16 [4096, 4096], P('vocab'), may hold values from -0.09375 to 0.09375
- final_gain: float32 [4096], replicated, may hold values from 0.5 to 1.5
- head_w: bfloat16 [8192, 4096], P('vocab', 'dp'), as said below
- targets: int32 [2, 1024], P(None, 'dp'), may hold values from 0 to 8191
- lengths: int32 [2], replicated, may hold values from 256 to 1024
Outputs:
- hidden_out: bfloat16 [2, 1024, 4096], P(None, 'dp', 'vocab')
- token_logp: float32 [2, 1024], P(None, 'dp')
- mean_logp: float32 [], replicated
Inputs may be any that keep to these rules, and one draw needn't show every extreme that they name: `head_w`: entries lie within 720 / sqrt(4096) of zero.
All inputs are finite; a program needn't handle non-finite values.
Results may differ from a plain program's by a relative error of at most 0.019.
Values may be sent and summed in bfloat16 or wider, within the bound.
A program may use at most 128 MiB of HBM per device.

v0:
```python
import math
import jax
import jax.numpy as jnp
from jax import lax
from jax.sharding import PartitionSpec as P


def shifted(array, axis, by):
    peers = lax.axis_size(axis)
    pairs = [(i, i + by) for i in range(peers) if 0 <= i + by < peers]
    return lax.ppermute(array, axis, pairs)


def prefix(part, axis, combine, identity):
    place = lax.axis_index(axis)
    gathered = jax.tree.map(lambda a: lax.all_gather(a, axis), part)
    state = jax.tree.map(lambda a, e: jnp.zeros_like(a) + jnp.asarray(e, a.dtype), part, identity)

    def one(step, state):
        return combine(
            state, jax.tree.map(lambda a: lax.dynamic_index_in_dim(a, step, 0, False), gathered)
        )

    return lax.fori_loop(0, place, one, state)


def rms_norm(values, gain, epsilon):
    return values * lax.rsqrt(jnp.mean(values * values, axis=-1, keepdims=True) + epsilon) * gain


def head_logits(final, head_w):
    return lax.dot_general(
        final,
        lax.all_gather(head_w, "dp", axis=1, tiled=True),
        (((1,), (1,)), ((), ())),
        preferred_element_type=jnp.float32,
    )


def body(
    resid,
    norm_gain,
    in_x,
    in_z,
    conv_w,
    conv_b,
    xdt_w,
    xbc_w,
    dt_gain,
    dt_proj,
    dt_bias,
    a_rate,
    out_w,
    final_gain,
    head_w,
    targets,
    lengths,
):
    batch_count, local_len, width = resid.shape
    channels = in_x.shape[1]
    nstate = a_rate.shape[1]
    kernel_len = conv_w.shape[0]
    row_count = batch_count * local_len
    stream = resid.astype(jnp.float32)
    normed = rms_norm(stream, norm_gain, 1e-05).astype(jnp.bfloat16).reshape(row_count, width)
    x_acc = jnp.dot(
        normed, lax.all_gather(in_x, "dp", axis=0, tiled=True), preferred_element_type=jnp.float32
    )
    z_acc = jnp.dot(
        normed, lax.all_gather(in_z, "dp", axis=0, tiled=True), preferred_element_type=jnp.float32
    )
    x_inner = x_acc.astype(jnp.bfloat16).reshape(batch_count, local_len, channels)
    z_gate = z_acc.astype(jnp.bfloat16).reshape(batch_count, local_len, channels)
    before = shifted(x_inner[:, local_len - (kernel_len - 1) :, :], "dp", 1)
    padded = jnp.concatenate([before, x_inner], axis=1).astype(jnp.float32)
    conv_sum = jnp.zeros((batch_count, local_len, channels), jnp.float32) + conv_b
    for tap_index in range(kernel_len):
        conv_sum = conv_sum + conv_w[tap_index] * padded[:, tap_index : tap_index + local_len, :]
    conv_act = jax.nn.silu(conv_sum)
    conv_low = conv_act.astype(jnp.bfloat16).reshape(row_count, channels)
    dt_raw, bc_raw = (
        lax.psum(
            jnp.dot(conv_low, xdt_w, preferred_element_type=jnp.float32).astype(jnp.bfloat16),
            "vocab",
        ).astype(jnp.float32),
        lax.psum(
            jnp.dot(conv_low, xbc_w, preferred_element_type=jnp.float32).astype(jnp.bfloat16),
            "vocab",
        ).astype(jnp.float32),
    )
    dt_normed = rms_norm(dt_raw, dt_gain, 1e-06).astype(jnp.bfloat16)
    step_size = jax.nn.softplus(
        jnp.dot(dt_normed, dt_proj, preferred_element_type=jnp.float32) + dt_bias
    ).reshape(batch_count, local_len, channels)
    in_map = bc_raw[:, :nstate].reshape(batch_count, local_len, nstate)
    out_map = bc_raw[:, nstate:].reshape(batch_count, local_len, nstate)
    block_len = math.gcd(local_len, 16)
    block_count = local_len // block_len

    def by_block(values):
        return values.transpose(1, 0, 2).reshape(
            (block_count, block_len) + (values.shape[0], values.shape[2])
        )

    def run_block(carry_state, inputs):
        step_blk, conv_blk, in_blk, out_blk = inputs
        results = []
        for position in range(block_len):
            carry_state = (
                jnp.exp(-step_blk[position][..., None] * a_rate) * carry_state
                + (step_blk[position] * conv_blk[position])[..., None]
                * in_blk[position][:, None, :]
            )
            results.append(jnp.sum(carry_state * out_blk[position][:, None, :], axis=-1))
        return (carry_state, jnp.stack(results))

    start_state = jnp.zeros((batch_count, channels, nstate), jnp.float32)
    last_state, local_out = lax.scan(
        run_block,
        start_state,
        (by_block(step_size), by_block(conv_act), by_block(in_map), by_block(out_map)),
    )
    local_out = local_out.reshape(local_len, batch_count, channels).transpose(1, 0, 2)
    step_total = jnp.sum(step_size, axis=1)
    last_decay = jnp.exp(-step_total[..., None] * a_rate)

    def chain(earlier, later):
        return (earlier[0] * later[0], later[0] * earlier[1] + later[1])

    _, state_in = prefix(
        (last_decay, last_state),
        "dp",
        chain,
        (jnp.ones_like(last_decay), jnp.zeros_like(last_state)),
    )
    step_cumul = jnp.cumsum(step_size, axis=1)
    carried = jnp.sum(
        out_map[:, :, None, :] * jnp.exp(-step_cumul[..., None] * a_rate) * state_in[:, None, :, :],
        axis=-1,
    )
    mixed = local_out + carried
    gated = (
        (mixed * jax.nn.silu(z_gate.astype(jnp.float32)))
        .astype(jnp.bfloat16)
        .reshape(row_count, channels)
    )
    partial_value = jnp.dot(gated, out_w, preferred_element_type=jnp.float32)
    vocab_count = lax.axis_size("vocab")
    vocab_index = lax.axis_index("vocab")
    share_width = width // vocab_count
    flat_stream = stream.reshape(row_count, width)
    mixer_out = lax.psum(partial_value.astype(jnp.bfloat16), "vocab").astype(jnp.float32)
    hidden = (flat_stream + mixer_out).astype(jnp.bfloat16)
    final = rms_norm(hidden.astype(jnp.float32), final_gain, 1e-05).astype(jnp.bfloat16)
    hidden_share = lax.dynamic_slice_in_dim(hidden, vocab_index * share_width, share_width, 1)
    logits = head_logits(final, head_w)
    vocab_rows = head_w.shape[0]
    local_ids = targets.reshape(row_count) - vocab_index * vocab_rows
    entry_ids = lax.broadcasted_iota(jnp.int32, (row_count, vocab_rows), 1)
    picked = jnp.sum(jnp.where(entry_ids == local_ids[:, None], logits, 0.0), axis=-1)
    local_top = jnp.max(logits, axis=-1)
    global_top = lax.pmax(local_top, "vocab")
    exp_local = jnp.sum(jnp.exp(logits - global_top[:, None]), axis=-1)
    exp_total, picked_all = lax.psum((exp_local, picked), "vocab")
    log_total = global_top + jnp.log(exp_total)
    token_logp = (picked_all - log_total).reshape(batch_count, local_len)
    positions = lax.axis_index("dp") * local_len + jnp.arange(local_len, dtype=jnp.int32)
    valid_mask = positions[None, :] < lengths[:, None]
    masked_sum = jnp.sum(jnp.where(valid_mask, token_logp, 0.0))
    grand_sum = lax.psum(masked_sum, "dp")
    mean_logp = grand_sum / jnp.sum(lengths.astype(jnp.float32))
    return (hidden_share.reshape(batch_count, local_len, share_width), token_logp, mean_logp)


def solution(mesh):
    in_specs = (
        P(None, "dp", None),
        P(),
        P("dp", "vocab"),
        P("dp", "vocab"),
        P(None, "vocab"),
        P("vocab"),
        P("vocab", None),
        P("vocab", None),
        P(),
        P(None, "vocab"),
        P("vocab"),
        P("vocab", None),
        P("vocab", None),
        P(),
        P("vocab", "dp"),
        P(None, "dp"),
        P(),
    )
    out_specs = (P(None, "dp", "vocab"), P(None, "dp"), P())
    return jax.shard_map(body, mesh=mesh, in_specs=in_specs, out_specs=out_specs, check_vma=False)
```

profile of v0, /device:TPU:0, one launch (start us, length us, event | category | flops | bytes accessed | tf_op | source)
XLA Modules:
  0.0 477.5 jit_solution(16889401138438752080)
XLA Ops:
  8.0 2.1 multiply_reduce_fusion.17
  10.1 2.7 multiply_convert_fusion
  12.8 54.1 %all-gather.7.cloned.1.call-done = bf16[4096,1024]{1,0:T(8,128)(2,1)} async-done(((bf16[512,1024]{1,0:T(8,128)(2,1)}), bf16[4096,1024]{1,0:T(8,128)(2,1)}) %all-gather.7.cloned.1.call-update) | async-done | bytes 8388624 | tf_op jit(solution)/shard_map/all_gather | solution.py:67
  66.9 6.4 %convolution_convert_fusion.2 = bf16[256,1024]{1,0:T(8,128)(2,1)S(1)} fusion(bf16[256,4096]{1,0:T(8,128)(2,1)} %bitcast.279, bf16[4096,1024]{1,0:T(8,128)(2,1)} %all-gather.7.cloned.1.call-done), kind=kOutput, calls=%fused_computation.218 | convolution fusion | flops 2147745792 | bytes 11010048 | tf_op jit(solution)/shard_map/dot_general | solution.py:66
  73.3 2.3 collective-permute-start
  76.6 1.7 fusion.75
  80.3 18.7 %psum.43 = bf16[256,32]{0,1:T(8,128)(2,1)S(1)} all-reduce(bf16[256,32]{0,1:T(8,128)(2,1)S(1)} %convolution_convert_fusion.4), channel_id=1, replica_groups=mesh['dp'=8,'vocab'=4] {'vocab'}, use_global_device_ids=true, to_apply=%region_3.4 | all-reduce | flops 8192 | bytes 32768 | tf_op jit(solution)/shard_map/psum | solution.py:86
  99.4 17.4 %all-reduce.4.cloned.1.call-done = bf16[256,256]{1,0:T(8,128)(2,1)} async-done(((bf16[256,256]{1,0:T(8,128)(2,1)}), bf16[256,256]{1,0:T(8,128)(2,1)}) %all-reduce.4.cloned.1.call-update) | async-done | bytes 131088 | tf_op jit(solution)/shard_map/psum | solution.py:82
  117.8 1.8 bitcast_reduce_fusion
  120.5 1.9 copy.36
  122.4 48.8 %while.26 = (s32[]{:T(128)}, f32[2,1024,16]{1,2,0:T(8,128)S(1)}, f32[8,16,2,1024]{3,1,0,2:T(8,128)}, f32[8,16,2,1024]{3,2,1,0:T(2,128)}, f32[1024,16]{0,1:T(8,12...) while((s32[]{:T(128)}, f32[2,1024,16]{1,2,0:T(8,128)S(1)}, ...), condition=%wide.region_21.22_spmd.clone, body=%wide.region_4.21_spmd.clone.sunk | while | flops 4816914 | bytes 3422816 | solution.py:118
  122.4 1.6 constant_dynamic-slice_fusion.66
  128.5 1.6 constant_dynamic-slice_fusion.66
  134.6 1.6 constant_dynamic-slice_fusion.66
  140.7 1.6 constant_dynamic-slice_fusion.66
  146.7 1.6 constant_dynamic-slice_fusion.66
  158.8 1.9 constant_dynamic-slice_fusion.66
  165.2 1.6 constant_dynamic-slice_fusion.66
  172.7 6.3 %convolution_convert_fusion.1 = bf16[256,1024]{1,0:T(8,128)(2,1)S(1)} fusion(bf16[256,4096]{1,0:T(8,128)(2,1)} %bitcast.280, bf16[4096,1024]{1,0:T(8,128)(2,1)} %all-gather.11.cloned.1.call-done), kind=kOutput, calls=%fused_computation.217 | convolution fusion | flops 2147745792 | bytes 11010048 | tf_op jit(solution)/shard_map/dot_general | solution.py:69
  179.2 2.7 reduce_window_sum.11
  181.9 2.3 neg.205
  184.3 13.5 %all-gather.15.cloned.1.call-done = f32[16,1024,16]{1,2,0:T(8,128)} async-done(((f32[2,1024,16]{1,2,0:T(8,128)}), f32[16,1024,16]{1,2,0:T(8,128)}) %all-gather.15.cloned.1.call-update) | async-done | bytes 1048592 | tf_op jit(solution)/shard_map/all_gather | solution.py:16
  197.8 25.7 %all-gather.9.cloned.1.call-done = f32[8,2,1024,16]{2,3,1,0:T(8,128)} async-done(((f32[1,2,1024,16]{2,3,1,0:T(8,128)}), f32[8,2,1024,16]{2,3,1,0:T(8,128)}) %all-gather.9.cloned.1.call-update) | async-done | bytes 1048592 | tf_op jit(solution)/shard_map/all_gather | solution.py:16
  223.7 6.2 %multiply_reduce_fusion.16 = f32[2,128,1024]{2,1,0:T(8,128)S(1)} fusion(f32[2,1024,16]{1,2,0:T(8,128)S(1)} %get-tuple-element.92, f32[1024,16]{0,1:T(8,128)S(1)} %get-tuple-element.677, f32[2,128,1024]{2,1,0:T(8,128)} %neg.205, f32[2,128,16]{2,1,0:T(8,128)S(1)} %copy.41), kind=kLoop, calls=%fused_computation.196 | loop fusion | flops 16515072 | bytes 2310144 | tf_op jit(solution)/shard_map/reduce_sum | solution.py:137
  230.3 7.0 %convolution_convert_fusion = bf16[256,4096]{1,0:T(8,128)(2,1)} fusion(bf16[256,1024]{1,0:T(8,128)(2,1)S(1)} %bitcast.285, bf16[1024,4096]{1,0:T(8,128)(2,1)} %param.33), kind=kOutput, calls=%fused_computation.199 | convolution fusion | flops 2148532224 | bytes 11010048 | tf_op jit(solution)/shard_map/dot_general | solution.py:147
  238.8 92.2 %all-reduce.6.cloned.1.call-done = bf16[256,4096]{1,0:T(8,128)(2,1)} async-done(((bf16[256,4096]{1,0:T(8,128)(2,1)}), bf16[256,4096]{1,0:T(8,128)(2,1)}) %all-reduce.6.cloned.1.call-update) | async-done | bytes 2097168 | tf_op jit(solution)/shard_map/psum | solution.py:152
  331.0 2.5 fusion.49
  335.7 89.2 %all-gather.13.cloned.1.call-done = bf16[2048,4096]{1,0:T(8,128)(2,1)} async-done(((bf16[2048,512]{1,0:T(8,128)(2,1)}), bf16[2048,4096]{1,0:T(8,128)(2,1)}) %all-gather.13.cloned.1.call-update) | async-done | bytes 16777232 | tf_op jit(solution)/shard_map/all_gather | solution.py:34
  424.9 9.0 %fusion.78 = (f32[256]{0:T(256)S(1)}, f32[256,2048]{1,0:T(8,128)S(1)}) fusion(bf16[2048,4096]{1,0:T(8,128)(2,1)} %all-gather.13.cloned.1.call-done, bf16[256,4096]{1,0:T(8,128)(2,1)} %copy-done.6, f32[4096]{0:T(1024)S(1)} %copy-done.14, f32[256]{0:T(256)S(1)} %add_rsqrt_fusion), kind=kOutput, calls=%fused_computation.260 | convolution fusion | flops 4299685888 | bytes 20989952 | tf_op jit(solution)/shard_map/dot_general | solution.py:32
  433.9 11.7 %pmax.7 = f32[256]{0:T(256)S(1)} all-reduce(f32[256]{0:T(256)S(1)} %get-tuple-element.288), channel_id=1, replica_groups=mesh['dp'=8,'vocab'=4] {'vocab'}, use_global_device_ids=true, to_apply=%region_32.33 | all-reduce | flops 256 | bytes 2048 | tf_op jit(solution)/shard_map/pmax | solution.py:162
  446.2 8.4 %all-reduce = (f32[256]{0:T(256)S(1)}, f32[256]{0:T(256)S(1)}) all-reduce(f32[256]{0:T(256)S(1)} %get-tuple-element.144, f32[256]{0:T(256)S(1)} %get-tuple-element.143), channel_id=1, replica_groups=mesh['dp'=8,'vocab'=4] {'vocab'}, use_global_device_ids=true, to_apply=%region_30.31 | all-reduce | flops 512 | bytes 4096 | tf_op jit(solution)/shard_map/psum | solution.py:164
  455.8 12.4 %psum.47 = f32[]{:T(128)} all-reduce(f32[]{:T(128)} %get-tuple-element.284), channel_id=1, replica_groups=mesh['dp'=8,'vocab'=4] {'dp'}, use_global_device_ids=true, to_apply=%region_36.37 | all-reduce | flops 1 | bytes 8 | tf_op jit(solution)/shard_map/psum | solution.py:170
  (279 shorter events, 50.0 us)
Async XLA Ops:
  7.2 110.6 %copy-start = (bf16[256,1024]{1,0:T(8,128)(2,1)S(1)}, bf16[256,1024]{1,0:T(8,128)(2,1)}, u32[]{:S(2)}) copy-start(bf16[256,1024]{1,0:T(8,128)(2,1)} %param.30) | copy-start | bytes 1572868
  7.2 2.9 copy-start.3
  7.2 59.7 %all-gather.7.cloned.1.call-start = ((), (), s32[]{:S(2)}) async-start(), calls=%async_computation | async-start | bytes 9437184 | tf_op jit(solution)/shard_map/all_gather | solution.py:67
  7.9 108.8 %all-reduce.4.cloned.1.call-start = ((), (), s32[]{:S(2)}) async-start(), calls=%async_computation.1 | async-start | bytes 262144 | tf_op jit(solution)/shard_map/psum | solution.py:82
  66.9 8.7 %copy-start.10 = (f32[4,1024]{1,0:T(4,128)S(1)}, f32[4,1024]{1,0:T(4,128)}, u32[]{:S(2)}) copy-start(f32[4,1024]{1,0:T(4,128)} %param.25) | copy-start | bytes 49156
  66.9 9.7 %copy-start.11 = (f32[1024]{0:T(1024)S(1)}, f32[1024]{0:T(1024)}, u32[]{:S(2)}) copy-start(f32[1024]{0:T(1024)} %param.26) | copy-start | bytes 12292
  73.3 5.0 %copy-start.8 = (bf16[1024,256]{1,0:T(8,128)(2,1)S(1)}, bf16[1024,256]{1,0:T(8,128)(2,1)}, u32[]{:S(2)}) copy-start(bf16[1024,256]{1,0:T(8,128)(2,1)} %param.27) | copy-start | bytes 1572868
  73.3 3.1 collective-permute-start
  76.6 3.5 copy-start.9
  76.6 41.2 %copy-start.15 = (f32[1024]{0:T(1024)S(1)}, f32[1024]{0:T(1024)}, u32[]{:S(2)}) copy-start(f32[1024]{0:T(1024)} %param.31) | copy-start | bytes 12292
  76.6 41.2 %copy-start.16 = (f32[256]{0:T(256)S(1)}, f32[256]{0:T(256)}, u32[]{:S(2)}) copy-start(f32[256]{0:T(256)} %param.29) | copy-start | bytes 3076
  79.3 43.2 %copy-start.2 = (f32[1024,16]{0,1:T(8,128)S(1)}, f32[1024,16]{0,1:T(8,128)}, u32[]{:S(2)}) copy-start(f32[1024,16]{0,1:T(8,128)} %param.32) | copy-start | bytes 196612
  79.3 93.4 %all-gather.11.cloned.1.call-start = ((), (), s32[]{:S(2)}) async-start(), calls=%async_computation.3 | async-start | bytes 9437184 | tf_op jit(solution)/shard_map/all_gather | solution.py:70
  80.0 117.7 %all-gather.15.cloned.1.call-start = ((), (), s32[]{:S(2)}) async-start(), calls=%async_computation.6 | async-start | bytes 1179648 | tf_op jit(solution)/shard_map/all_gather | solution.py:16
  119.6 1.0 copy-start.5
  171.2 0.6 copy-start.4
  171.9 51.6 %all-gather.9.cloned.1.call-start = ((), (), s32[]{:S(2)}) async-start(), calls=%async_computation.2 | async-start | bytes 1179648 | tf_op jit(solution)/shard_map/all_gather | solution.py:16
  172.6 158.3 %all-reduce.6.cloned.1.call-start = ((), (), s32[]{:S(2)}) async-start(), calls=%async_computation.4 | async-start | bytes 4194304 | tf_op jit(solution)/shard_map/psum | solution.py:152
  223.7 6.3 %copy-start.7 = (f32[8,16,2,1024]{3,1,0,2:T(8,128)S(1)}, f32[8,16,2,1024]{3,1,0,2:T(8,128)}, u32[]{:S(2)}) copy-start(f32[8,16,2,1024]{3,1,0,2:T(8,128)} %get-tuple-element.90) | copy-start | bytes 3145732
  237.3 0.8 copy-start.13
  237.3 1.5 copy-start.12
  237.4 187.6 %all-gather.13.cloned.1.call-start = ((), (), s32[]{:S(2)}) async-start(), calls=%async_computation.5 | async-start | bytes 18874368 | tf_op jit(solution)/shard_map/all_gather | solution.py:34
  238.1 186.8 %copy-start.14 = (f32[4096]{0:T(1024)S(1)}, f32[4096]{0:T(1024)}, u32[]{:S(2)}) copy-start(f32[4096]{0:T(1024)} %param.34) | copy-start | bytes 49156
  333.5 1.4 copy-start.6
  424.9 44.6 %copy-start.1 = (bf16[256,1024]{1,0:T(8,128)(2,1)S(1)}, bf16[256,1024]{1,0:T(8,128)(2,1)}, u32[]{:S(2)}) copy-start(bf16[256,1024]{1,0:T(8,128)(2,1)} %param.30) | copy-start | bytes 1572868
Sparse Core Ops, SparseCore 0:
  9.9 56.9 all-gather.6
  79.4 37.2 all-reduce.3
  118.6 53.9 all-gather.10
  174.4 23.3 all-gather.14
  200.1 23.3 all-gather.8
  237.5 93.4 all-reduce.5
  332.8 92.0 all-gather.12
where the time goes:
time: 480 us; the launch traced here: 478 us
  waiting for transfers between devices  295 us (61%)
  other arithmetic  51.9 us (11%)
  blocking collectives  51.3 us (11%)
  matrix products  31.7 us (7%)
  local copies, waits for them, and re-layouts  27.4 us (6%)
  between operations  16.9 us (4%)
    psum x1, waiting for transfers between devices, body(): lax.psum(partial_value.astype(jnp.bfloat16), 'vocab').astype(jnp.float32)  92.2 us
    all_gather x1, waiting for transfers between devices, head_logits(): lax.all_gather(head_w, 'dp', axis=1, tiled=True)  89.2 us
    all_gather x1, waiting for transfers between devices, body(): lax.all_gather(in_x, 'dp', axis=0, tiled=True)  54.1 us
    all_gather x2, waiting for transfers between devices, prefix(): gathered = jax.tree.map(lambda a: lax.all_gather(a, axis), part)  39.2 us
    psum x1, blocking collectives, body(): lax.psum(jnp.dot(conv_low, xbc_w, preferred_element_type=jnp.float32).ast...  18.7 us
    psum x1, waiting for transfers between devices, body(): lax.psum(jnp.dot(conv_low, xdt_w, preferred_element_type=jnp.float32).ast...  17.4 us
    neg x16, other arithmetic, run_block(): -step_blk[position][..., None] * a_rate  14.9 us
    slice x8, local copies, waits for them, and re-layouts, run_block(): conv_blk[position]  13.3 us
  transfers between devices with their start and end apart: 8, of which 7 were waited for; matrix products, arithmetic and copies ran while one was open for 16% of the time, Pallas kernels for 0%

commit v1 on v0

--- a/solution.py
+++ b/solution.py
@@ -3,6 +3,11 @@
 import jax.numpy as jnp
 from jax import lax
 from jax.sharding import PartitionSpec as P
+
+
+def gather_and_add(x, mesh_axis):
+    parts = lax.all_gather(x, mesh_axis)
+    return jnp.sum(parts, axis=0)
 
 
 def shifted(array, axis, by):
@@ -149,7 +154,7 @@
     vocab_index = lax.axis_index("vocab")
     share_width = width // vocab_count
     flat_stream = stream.reshape(row_count, width)
-    mixer_out = lax.psum(partial_value.astype(jnp.bfloat16), "vocab").astype(jnp.float32)
+    mixer_out = gather_and_add(partial_value.astype(jnp.bfloat16), "vocab").astype(jnp.float32)
     hidden = (flat_stream + mixer_out).astype(jnp.bfloat16)
     final = rms_norm(hidden.astype(jnp.float32), final_gain, 1e-05).astype(jnp.bfloat16)
     hidden_share = lax.dynamic_slice_in_dim(hidden, vocab_index * share_width, share_width, 1)

time: 480 us -> 542 us (1.13)
  waiting for transfers between devices: 295 us -> 351 us
  other arithmetic: 51.9 us -> 59.9 us
    all_gather x0 -> x1, waiting for transfers between devices: none -> 156 us  [gather_and_add(): parts = lax.all_gather(x, mesh_axis)]
    psum x1 -> x0, waiting for transfers between devices: 92.2 us -> none  [body(): lax.psum(partial_value.astype(jnp.bfloat16), 'vocab').astype(jnp.float32)]
    all_gather x1, waiting for transfers between devices: 89.2 us -> 81.5 us  [head_logits(): lax.all_gather(head_w, 'dp', axis=1, tiled=True)]
    reduce_sum x0 -> x1, other arithmetic: none -> 6.96 us  [gather_and_add(): return jnp.sum(parts, axis=0)]
  transfers between devices with their start and end apart: 8 -> 8, of which waited for: 7 -> 7; matrix products, arithmetic and copies ran while one was open for 16% -> 15% of each run, Pallas kernels for 0% -> 0%
where the time goes in v1:
time: 542 us; the launch traced here: 540 us
  waiting for transfers between devices  351 us (65%)
  other arithmetic  59.9 us (11%)
  blocking collectives  51.3 us (9%)
  matrix products  31.8 us (6%)
  local copies, waits for them, and re-layouts  26.2 us (5%)
  between operations  16.8 us (3%)
    all_gather x1, waiting for transfers between devices, gather_and_add(): parts = lax.all_gather(x, mesh_axis)  156 us
    all_gather x1, waiting for transfers between devices, head_logits(): lax.all_gather(head_w, 'dp', axis=1, tiled=True)  81.5 us
    all_gather x1, waiting for transfers between devices, body(): lax.all_gather(in_x, 'dp', axis=0, tiled=True)  54.1 us
    all_gather x2, waiting for transfers between devices, prefix(): gathered = jax.tree.map(lambda a: lax.all_gather(a, axis), part)  39.2 us
    psum x1, blocking collectives, body(): lax.psum(jnp.dot(conv_low, xbc_w, preferred_element_type=jnp.float32).ast...  18.7 us
    psum x1, waiting for transfers between devices, body(): lax.psum(jnp.dot(conv_low, xdt_w, preferred_element_type=jnp.float32).ast...  17.4 us
    neg x16, other arithmetic, run_block(): -step_blk[position][..., None] * a_rate  14.9 us
    slice x8, local copies, waits for them, and re-layouts, run_block(): conv_blk[position]  13.3 us
  transfers between devices with their start and end apart: 8, of which 7 were waited for; matrix products, arithmetic and copies ran while one was open for 15% of the time, Pallas kernels for 0%

profile of v1, /device:TPU:0, one launch (start us, length us, event | category | flops | bytes accessed | tf_op | source)
XLA Modules:
  0.0 540.2 jit_solution(740739931242244088)
XLA Ops:
  8.0 2.1 multiply_reduce_fusion.18
  10.1 2.7 multiply_convert_fusion.1
  12.8 54.1 %all-gather.9.cloned.1.call-done = bf16[4096,1024]{1,0:T(8,128)(2,1)} async-done(((bf16[512,1024]{1,0:T(8,128)(2,1)}), bf16[4096,1024]{1,0:T(8,128)(2,1)}) %all-gather.9.cloned.1.call-update) | async-done | bytes 8388624 | tf_op jit(solution)/shard_map/all_gather | solution.py:72
  66.9 6.4 %convolution_convert_fusion.2 = bf16[256,1024]{1,0:T(8,128)(2,1)S(1)} fusion(bf16[256,4096]{1,0:T(8,128)(2,1)} %bitcast.285, bf16[4096,1024]{1,0:T(8,128)(2,1)} %all-gather.9.cloned.1.call-done), kind=kOutput, calls=%fused_computation.216 | convolution fusion | flops 2147745792 | bytes 11010048 | tf_op jit(solution)/shard_map/dot_general | solution.py:71
  73.3 2.3 collective-permute-start
  76.6 1.7 fusion.70
  80.3 18.7 %psum.36 = bf16[256,32]{0,1:T(8,128)(2,1)S(1)} all-reduce(bf16[256,32]{0,1:T(8,128)(2,1)S(1)} %convolution_convert_fusion.4), channel_id=1, replica_groups=mesh['dp'=8,'vocab'=4] {'vocab'}, use_global_device_ids=true, to_apply=%region_3.4 | all-reduce | flops 8192 | bytes 32768 | tf_op jit(solution)/shard_map/psum | solution.py:91
  99.4 17.4 %all-reduce.3.cloned.1.call-done = bf16[256,256]{1,0:T(8,128)(2,1)} async-done(((bf16[256,256]{1,0:T(8,128)(2,1)}), bf16[256,256]{1,0:T(8,128)(2,1)}) %all-reduce.3.cloned.1.call-update) | async-done | bytes 131088 | tf_op jit(solution)/shard_map/psum | solution.py:87
  117.8 1.8 bitcast_reduce_fusion
  120.5 1.9 copy.36
  122.4 48.8 %while.26 = (s32[]{:T(128)}, f32[2,1024,16]{1,2,0:T(8,128)S(1)}, f32[8,16,2,1024]{3,1,0,2:T(8,128)}, f32[8,16,2,1024]{3,2,1,0:T(2,128)}, f32[1024,16]{0,1:T(8,12...) while((s32[]{:T(128)}, f32[2,1024,16]{1,2,0:T(8,128)S(1)}, ...), condition=%wide.region_21.22_spmd.clone, body=%wide.region_4.21_spmd.clone.sunk | while | flops 4816914 | bytes 3422816 | solution.py:123
  122.4 1.6 constant_dynamic-slice_fusion.66
  128.5 1.6 constant_dynamic-slice_fusion.66
  134.6 1.6 constant_dynamic-slice_fusion.66
  140.7 1.6 constant_dynamic-slice_fusion.66
  158.8 1.9 constant_dynamic-slice_fusion.66
  165.2 1.6 constant_dynamic-slice_fusion.66
  172.7 6.3 %convolution_convert_fusion.1 = bf16[256,1024]{1,0:T(8,128)(2,1)S(1)} fusion(bf16[256,4096]{1,0:T(8,128)(2,1)} %bitcast.286, bf16[4096,1024]{1,0:T(8,128)(2,1)} %all-gather.13.cloned.1.call-done), kind=kOutput, calls=%fused_computation.215 | convolution fusion | flops 2147745792 | bytes 11010048 | tf_op jit(solution)/shard_map/dot_general | solution.py:74
  179.2 2.7 reduce_window_sum.11
  181.9 2.3 neg.205
  184.3 13.5 %all-gather.17.cloned.1.call-done = f32[16,1024,16]{1,2,0:T(8,128)} async-done(((f32[2,1024,16]{1,2,0:T(8,128)}), f32[16,1024,16]{1,2,0:T(8,128)}) %all-gather.17.cloned.1.call-update) | async-done | bytes 1048592 | tf_op jit(solution)/shard_map/all_gather | solution.py:21
  197.8 25.7 %all-gather.11.cloned.1.call-done = f32[8,2,1024,16]{2,3,1,0:T(8,128)} async-done(((f32[1,2,1024,16]{2,3,1,0:T(8,128)}), f32[8,2,1024,16]{2,3,1,0:T(8,128)}) %all-gather.11.cloned.1.call-update) | async-done | bytes 1048592 | tf_op jit(solution)/shard_map/all_gather | solution.py:21
  223.7 6.2 %multiply_reduce_fusion.16 = f32[2,128,1024]{2,1,0:T(8,128)S(1)} fusion(f32[2,1024,16]{1,2,0:T(8,128)S(1)} %get-tuple-element.92, f32[1024,16]{0,1:T(8,128)S(1)} %get-tuple-element.675, f32[2,128,1024]{2,1,0:T(8,128)} %neg.205, f32[2,128,16]{2,1,0:T(8,128)S(1)} %copy.41), kind=kLoop, calls=%fused_computation.196 | loop fusion | flops 16515072 | bytes 2310144 | tf_op jit(solution)/shard_map/reduce_sum | solution.py:142
  230.3 7.1 %convolution_convert_fusion = bf16[256,4096]{1,0:T(8,128)(2,1)} fusion(bf16[256,1024]{1,0:T(8,128)(2,1)S(1)} %bitcast.291, bf16[1024,4096]{1,0:T(8,128)(2,1)} %param.33), kind=kOutput, calls=%fused_computation.197 | convolution fusion | flops 2148532224 | bytes 11010048 | tf_op jit(solution)/shard_map/dot_general | solution.py:152
  238.8 155.7 %all-gather.19.cloned.1.call-done = bf16[1024,4096]{1,0:T(8,128)(2,1)} async-done(((bf16[256,4096]{1,0:T(8,128)(2,1)}), bf16[1024,4096]{1,0:T(8,128)(2,1)}) %all-gather.19.cloned.1.call-update) | async-done | bytes 8388624 | tf_op jit(solution)/shard_map/all_gather | solution.py:9
  394.5 7.0 %reduce_sum.241 = bf16[256,4096]{1,0:T(8,128)(2,1)} reduce(bf16[4,256,4096]{2,1,0:T(8,128)(2,1)} %bitcast.277, bf16[]{:T(256)} %constant.71.clone.1), dimensions={0}, to_apply=%region_27.28 | reduce | flops 3145728 | bytes 10485762 | tf_op jit(solution)/shard_map/reduce_sum | solution.py:10
  401.5 2.9 fusion.49
  406.2 81.5 %all-gather.15.cloned.1.call-done = bf16[2048,4096]{1,0:T(8,128)(2,1)} async-done(((bf16[2048,512]{1,0:T(8,128)(2,1)}), bf16[2048,4096]{1,0:T(8,128)(2,1)}) %all-gather.15.cloned.1.call-update) | async-done | bytes 16777232 | tf_op jit(solution)/shard_map/all_gather | solution.py:39
  487.6 9.0 %fusion.73 = (f32[256]{0:T(256)S(1)}, f32[256,2048]{1,0:T(8,128)S(1)}) fusion(bf16[2048,4096]{1,0:T(8,128)(2,1)} %all-gather.15.cloned.1.call-done, bf16[256,4096]{1,0:T(8,128)(2,1)} %copy-done.7, f32[4096]{0:T(1024)S(1)} %copy-done.15, f32[256]{0:T(256)S(1)} %rsqrt_bitcast_fusion), kind=kOutput, calls=%fused_computation.258 | convolution fusion | flops 4299685888 | bytes 20989952 | tf_op jit(solution)/shard_map/dot_general | solution.py:37
  496.6 11.7 %pmax.7 = f32[256]{0:T(256)S(1)} all-reduce(f32[256]{0:T(256)S(1)} %get-tuple-element.286), channel_id=1, replica_groups=mesh['dp'=8,'vocab'=4] {'vocab'}, use_global_device_ids=true, to_apply=%region_32.33 | all-reduce | flops 256 | bytes 2048 | tf_op jit(solution)/shard_map/pmax | solution.py:167
  509.0 8.4 %all-reduce = (f32[256]{0:T(256)S(1)}, f32[256]{0:T(256)S(1)}) all-reduce(f32[256]{0:T(256)S(1)} %get-tuple-element.144, f32[256]{0:T(256)S(1)} %get-tuple-element.143), channel_id=1, replica_groups=mesh['dp'=8,'vocab'=4] {'vocab'}, use_global_device_ids=true, to_apply=%region_30.31 | all-reduce | flops 512 | bytes 4096 | tf_op jit(solution)/shard_map/psum | solution.py:169
  518.5 12.4 %psum.39 = f32[]{:T(128)} all-reduce(f32[]{:T(128)} %get-tuple-element.282), channel_id=1, replica_groups=mesh['dp'=8,'vocab'=4] {'dp'}, use_global_device_ids=true, to_apply=%region_36.37 | all-reduce | flops 1 | bytes 8 | tf_op jit(solution)/shard_map/psum | solution.py:175
  (283 shorter events, 51.1 us)
Async XLA Ops:
  7.2 110.6 %copy-start = (bf16[256,1024]{1,0:T(8,128)(2,1)S(1)}, bf16[256,1024]{1,0:T(8,128)(2,1)}, u32[]{:S(2)}) copy-start(bf16[256,1024]{1,0:T(8,128)(2,1)} %param.30) | copy-start | bytes 1572868
  7.2 2.9 copy-start.3
  7.2 59.7 %all-gather.9.cloned.1.call-start = ((), (), s32[]{:S(2)}) async-start(), calls=%async_computation | async-start | bytes 9437184 | tf_op jit(solution)/shard_map/all_gather | solution.py:72
  7.9 108.8 %all-reduce.3.cloned.1.call-start = ((), (), s32[]{:S(2)}) async-start(), calls=%async_computation.1 | async-start | bytes 262144 | tf_op jit(solution)/shard_map/psum | solution.py:87
  66.9 8.7 %copy-start.11 = (f32[4,1024]{1,0:T(4,128)S(1)}, f32[4,1024]{1,0:T(4,128)}, u32[]{:S(2)}) copy-start(f32[4,1024]{1,0:T(4,128)} %param.25) | copy-start | bytes 49156
  66.9 9.7 %copy-start.12 = (f32[1024]{0:T(1024)S(1)}, f32[1024]{0:T(1024)}, u32[]{:S(2)}) copy-start(f32[1024]{0:T(1024)} %param.26) | copy-start | bytes 12292
  73.3 5.0 copy-start.9
  73.3 3.1 collective-permute-start
  76.6 3.5 copy-start.10
  76.6 41.2 %copy-start.16 = (f32[1024]{0:T(1024)S(1)}, f32[1024]{0:T(1024)}, u32[]{:S(2)}) copy-start(f32[1024]{0:T(1024)} %param.31) | copy-start | bytes 12292
  76.6 41.2 %copy-start.17 = (f32[256]{0:T(256)S(1)}, f32[256]{0:T(256)}, u32[]{:S(2)}) copy-start(f32[256]{0:T(256)} %param.29) | copy-start | bytes 3076
  79.3 43.2 %copy-start.2 = (f32[1024,16]{0,1:T(8,128)S(1)}, f32[1024,16]{0,1:T(8,128)}, u32[]{:S(2)}) copy-start(f32[1024,16]{0,1:T(8,128)} %param.32) | copy-start | bytes 196612
  79.3 93.4 %all-gather.13.cloned.1.call-start = ((), (), s32[]{:S(2)}) async-start(), calls=%async_computation.3 | async-start | bytes 9437184 | tf_op jit(solution)/shard_map/all_gather | solution.py:75
  80.0 117.7 %all-gather.17.cloned.1.call-start = ((), (), s32[]{:S(2)}) async-start(), calls=%async_computation.5 | async-start | bytes 1179648 | tf_op jit(solution)/shard_map/all_gather | solution.py:21
  119.6 1.0 copy-start.6
  171.2 0.6 copy-start.5
  171.9 51.6 %all-gather.11.cloned.1.call-start = ((), (), s32[]{:S(2)}) async-start(), calls=%async_computation.2 | async-start | bytes 1179648 | tf_op jit(solution)/shard_map/all_gather | solution.py:21
  172.6 221.9 %all-gather.19.cloned.1.call-start = ((), (), s32[]{:S(2)}) async-start(), calls=%async_computation.6 | async-start | bytes 10485760 | tf_op jit(solution)/shard_map/all_gather | solution.py:9
  223.7 6.3 %copy-start.8 = (f32[8,16,2,1024]{3,1,0,2:T(8,128)S(1)}, f32[8,16,2,1024]{3,1,0,2:T(8,128)}, u32[]{:S(2)}) copy-start(f32[8,16,2,1024]{3,1,0,2:T(8,128)} %get-tuple-element.90) | copy-start | bytes 3145732
  237.4 0.8 copy-start.14
  237.4 1.4 copy-start.13
  237.5 250.2 %all-gather.15.cloned.1.call-start = ((), (), s32[]{:S(2)}) async-start(), calls=%async_computation.4 | async-start | bytes 18874368 | tf_op jit(solution)/shard_map/all_gather | solution.py:39
  401.5 3.9 copy-start.4
  404.4 1.7 copy-start.7
  404.4 83.2 %copy-start.15 = (f32[4096]{0:T(1024)S(1)}, f32[4096]{0:T(1024)}, u32[]{:S(2)}) copy-start(f32[4096]{0:T(1024)} %param.34) | copy-start | bytes 49156
  487.6 44.6 %copy-start.1 = (bf16[256,1024]{1,0:T(8,128)(2,1)S(1)}, bf16[256,1024]{1,0:T(8,128)(2,1)}, u32[]{:S(2)}) copy-start(bf16[256,1024]{1,0:T(8,128)(2,1)} %param.30) | copy-start | bytes 1572868
Sparse Core Ops, SparseCore 0:
  9.9 56.9 all-gather.8
  79.4 37.2 all-reduce.2
  118.6 53.9 all-gather.12
  174.4 23.3 all-gather.16
  200.1 23.3 all-gather.10
  237.6 156.8 all-gather.18
  396.4 91.1 all-gather.14
